TPU v7x, 32 devices: a whole 2x2x4 slice. The times are simulated.
32 devices in a mesh: row: 2 (over y), col: 4 (over z), depth: 4 (over x, core).
Axes of the slice: x: 2, y: 2, z: 4, core: 2. Of those that a mesh axis runs over, the one named last changes fastest.
Arguments:
- grad_out: bfloat16 [1024, 6144], P('depth', 'col'), may hold values from -6 to 6
- pre_act: bfloat16 [1024, 24576], P('depth', 'row'), may hold values from -8 to 8
- down_weight: bfloat16 [24576, 6144], P(('row', 'depth'), 'col'), may hold values from -0.0546875 to 0.0546875
Outputs:
- grad_pre: bfloat16 [1024, 24576], P('depth', 'row')
- grad_weight: bfloat16 [24576, 6144], P(('row', 'depth'), 'col')
All inputs are finite; a program needn't handle non-finite values.
Results may differ from a plain program's by a relative error of at most 0.0066.
Values may be sent and summed in bfloat16 or wider, within the bound.
A program may use at most 128 MiB of HBM per device.

v0:
```python
import jax
import jax.numpy as jnp
from jax import lax
from jax.sharding import PartitionSpec as P

sqrt_two_pi = 0.7978845608028654
cubic_coeff = 0.044715


def gelu_value(preact):
    tangent = jnp.tanh(sqrt_two_pi * (preact + cubic_coeff * preact * preact * preact))
    return 0.5 * preact * (1.0 + tangent)


def gelu_slope(preact):
    tangent = jnp.tanh(sqrt_two_pi * (preact + cubic_coeff * preact * preact * preact))
    inner = sqrt_two_pi * (1.0 + 3.0 * cubic_coeff * preact * preact)
    return 0.5 * (1.0 + tangent) + 0.5 * preact * (1.0 - tangent * tangent) * inner


def contract_last(left, right):
    return lax.dot_general(
        left, right, (((1,), (1,)), ((), ())), preferred_element_type=jnp.float32
    )


def contract_first(left, right):
    return lax.dot_general(
        left, right, (((0,), (0,)), ((), ())), preferred_element_type=jnp.float32
    )


def finish_rows(partial_value, preacts):
    total = lax.psum(partial_value, "col")
    return (total * gelu_slope(preacts.astype(jnp.float32))).astype(jnp.bfloat16)


def on_device(grad_out, pre_act, down_weight):
    every_grad = lax.all_gather(grad_out, "depth", axis=0, tiled=True)
    own_pre = lax.all_to_all(pre_act, "depth", split_axis=1, concat_axis=0, tiled=True)
    partial_value = contract_last(every_grad, down_weight)
    local_grad = finish_rows(partial_value, own_pre)
    grad_pre = lax.all_to_all(local_grad, "depth", split_axis=0, concat_axis=1, tiled=True)
    own_act = gelu_value(own_pre.astype(jnp.float32)).astype(jnp.bfloat16)
    grad_weight = contract_first(own_act, every_grad).astype(jnp.bfloat16)
    return (grad_pre, grad_weight)


def solution(mesh):
    placed = (P("depth", "col"), P("depth", "row"), P(("row", "depth"), "col"))
    return jax.shard_map(
        on_device,
        mesh=mesh,
        in_specs=placed,
        out_specs=(P("depth", "row"), P(("row", "depth"), "col")),
        check_vma=False,
    )
```

profile of v0, /device:TPU:0, one launch (start us, length us, event | category | flops | bytes accessed | tf_op | source)
XLA Modules:
  0.0 588.5 jit_solution(14912220487641829081)
XLA Ops:
  7.2 0.0 all-gather.2.cloned.1.call-start
  7.2 0.7 all-gather.2.cloned.1.call-update
  7.9 0.0 all-reduce.2.cloned.1.call-start
  7.9 32.8 %all-gather.2.cloned.1.call-done = bf16[1024,1536]{1,0:T(8,128)(2,1)} async-done(((bf16[256,1536]{1,0:T(8,128)(2,1)}), bf16[1024,1536]{1,0:T(8,128)(2,1)}) %all-gather.2.cloned.1.call-update) | async-done | bytes 3145744 | tf_op jit(solution)/shard_map/all_gather | solution.py:39
  40.8 16.2 %fusion.11 = f32[1024,3072]{1,0:T(8,128)} fusion(bf16[1024,1536]{1,0:T(8,128)(2,1)} %all-gather.2.cloned.1.call-done, bf16[3072,1536]{1,0:T(8,128)(2,1)} %param.5), kind=kOutput, calls=%fused_computation.16 | convolution fusion | flops 9663676416 | bytes 25165824 | tf_op jit(solution)/shard_map/dot_general | solution.py:22
  57.0 0.0 all-reduce.2.cloned.1.call-update
  57.0 3.2 copy.10
  60.2 74.3 %all_to_all.32 = bf16[256,4,3072]{2,0,1:T(8,128)(2,1)} all-to-all(bf16[256,4,3072]{2,0,1:T(8,128)(2,1)S(1)} %bitcast.30), channel_id=1, replica_groups=mesh['row'=2,'col'=4,'depth'=4] {'depth'}, dimensions={1} | all-to-all | bytes 12582912 | tf_op jit(solution)/shard_map/all_to_all | solution.py:40
  134.5 348.8 %all-reduce.2.cloned.1.call-done = f32[1024,3072]{1,0:T(8,128)} async-done(((f32[1024,3072]{1,0:T(8,128)}), f32[1024,3072]{1,0:T(8,128)}) %all-reduce.2.cloned.1.call-update) | async-done | bytes 12582928 | tf_op jit(solution)/shard_map/psum | solution.py:34
  483.3 16.1 %fusion.10 = (bf16[1024,3072]{1,0:T(8,128)(2,1)}, bf16[1024,3072]{1,0:T(8,128)(2,1)}) fusion(bf16[256,4,3072]{2,0,1:T(8,128)(2,1)} %all_to_all.32, f32[1024,3072]{1,0:T(8,128)} %all-reduce.2.cloned.1.call-done), kind=kLoop, calls=%fused_computation.13 | loop fusion | flops 69206016 | bytes 31457280 | tf_op jit(solution)/shard_map/convert_element_type | solution.py:44
  499.4 0.0 copy-start
  499.4 5.5 all-to-all-start.1
  504.9 0.0 copy-done
  504.9 14.9 %convolution_convert_fusion = bf16[3072,1536]{1,0:T(8,128)(2,1)} fusion(bf16[1024,3072]{1,0:T(8,128)(2,1)} %get-tuple-element.2, bf16[1024,1536]{1,0:T(8,128)(2,1)S(1)} %copy-done), kind=kOutput, calls=%fused_computation.14 | convolution fusion | flops 9668395008 | bytes 18874368 | tf_op jit(solution)/shard_map/dot_general | solution.py:28
  519.8 55.7 %all-to-all-done.1 = bf16[4,256,3072]{2,1,0:T(8,128)(2,1)} async-done(((bf16[4,256,3072]{2,1,0:T(8,128)(2,1)}), bf16[4,256,3072]{2,1,0:T(8,128)(2,1)}, u32[]{:S(2)}, u32[]{:S(2)}) %all-to-all-start.1) | async-done | bytes 6291488 | tf_op jit(solution)/shard_map/all_to_all | solution.py:43
  575.6 6.1 %copy.8 = bf16[4,32,8,3072]{3,2,0,1:T(8,128)(2,1)} copy(bf16[4,32,8,3072]{3,2,1,0:T(8,128)(2,1)} %bitcast.7) | data formatting | bytes 12582912 | tf_op jit(solution)/shard_map/all_to_all | solution.py:43
Async XLA Ops:
  7.2 33.6 %all-gather.2.cloned.1.call-start = ((), (), s32[]{:S(2)}) async-start(), calls=%async_computation.2 | async-start | bytes 3932160 | tf_op jit(solution)/shard_map/all_gather | solution.py:39
  7.9 475.4 %all-reduce.2.cloned.1.call-start = ((), (), s32[]{:S(2)}) async-start(), calls=%async_computation.3 | async-start | bytes 25165824 | tf_op jit(solution)/shard_map/psum | solution.py:34
  499.4 5.5 copy-start
  499.4 76.2 %all-to-all-start.1 = ((bf16[4,256,3072]{2,1,0:T(8,128)(2,1)}), bf16[4,256,3072]{2,1,0:T(8,128)(2,1)}, u32[]{:S(2)}, u32[]{:S(2)}) async-start(bf16[4,256,3072]{2,1,0:T(8,128)(2,1)} %bitcast.31), calls=%async_computation.1 | async-start | bytes 12582912 | tf_op jit(solution)/shard_map/all_to_all | solution.py:43
Sparse Core Ops, SparseCore 0:
  9.5 31.2 all-gather.1
  57.1 426.1 all-reduce.1
where the time goes:
time: 589 us
  waiting for transfers between devices  438 us (74%)
  blocking collectives  74.3 us (13%)
  matrix products  31.1 us (5%)
  other arithmetic  16.1 us (3%)
  between operations  14.1 us (2%)
  local copies, waits for them, and re-layouts  9.36 us (2%)
    psum x1, waiting for transfers between devices, finish_rows(): total = lax.psum(partial_value, 'col')  349 us
    all_to_all x1, blocking collectives, on_device(): lax.all_to_all(pre_act, 'depth', split_axis=1, concat_axis=0, tiled=True)  74.3 us
    all_to_all x1, waiting for transfers between devices, on_device(): lax.all_to_all(local_grad, 'depth', split_axis=0, concat_axis=1, tiled=True)  55.7 us
    all_gather x1, waiting for transfers between devices, on_device(): every_grad = lax.all_gather(grad_out, 'depth', axis=0, tiled=True)  32.8 us
    dot_general x1, matrix products, contract_last(): lax.dot_general(left, right, (((1,), (1,)), ((), ())), preferred_element_...  16.2 us
    convert_element_type x1, other arithmetic, on_device(): own_act = gelu_value(own_pre.astype(jnp.float32)).astype(jnp.bfloat16)  16.1 us
    dot_general x1, matrix products, contract_first(): lax.dot_general(left, right, (((0,), (0,)), ((), ())), preferred_element_...  14.9 us
  transfers between devices with their start and end apart: 3, of which 3 were waited for; matrix products, arithmetic and copies ran while one was open for 3% of the time, Pallas kernels for 0%

commit v1 on v0

--- a/solution.py
+++ b/solution.py
@@ -31,7 +31,8 @@
 
 
 def finish_rows(partial_value, preacts):
-    total = lax.psum(partial_value, "col")
+    passed = jax.lax.all_gather(partial_value, axis_name="col")
+    total = jnp.sum(passed, 0)
     return (total * gelu_slope(preacts.astype(jnp.float32))).astype(jnp.bfloat16)
 
 

time: 589 us -> 1030 us (1.75)
  waiting for transfers between devices: 438 us -> 898 us
  blocking collectives: 74.3 us -> 0 us
  other arithmetic: 16.1 us -> 43.3 us
  local copies, waits for them, and re-layouts: 9.36 us -> 35.9 us
    all_gather x0 -> x1, waiting for transfers between devices: none -> 812 us  [finish_rows(): passed = jax.lax.all_gather(partial_value, axis_name='col')]
    psum x1 -> x0, waiting for transfers between devices: 349 us -> none  [finish_rows(): total = lax.psum(partial_value, 'col')]
    all_to_all x1 -> x0, blocking collectives: 74.3 us -> none  [on_device(): lax.all_to_all(pre_act, 'depth', split_axis=1, concat_axis=0, tiled=True)]
    reduce_sum x0 -> x1, other arithmetic: none -> 23.9 us  [finish_rows(): total = jnp.sum(passed, 0)]
    unnamed x2 -> x4, local copies, waits for them, and re-layouts: 0.01 us -> 17.4 us
    convert_element_type x0 -> x1, other arithmetic: none -> 13.3 us  [finish_rows(): (total * gelu_slope(preacts.astype(jnp.float32))).astype(jnp.bfloat16)]
  transfers between devices with their start and end apart: 3 -> 4, of which waited for: 3 -> 3; matrix products, arithmetic and copies ran while one was open for 3% -> 6% of each run, Pallas kernels for 0% -> 0%
where the time goes in v1:
time: 1030 us
  waiting for transfers between devices  898 us (87%)
  other arithmetic  43.3 us (4%)
  local copies, waits for them, and re-layouts  35.9 us (3%)
  matrix products  28.3 us (3%)
  between operations  14.1 us (1%)
  starting transfers between devices  11.3 us (1%)
    all_gather x1, waiting for transfers between devices, finish_rows(): passed = jax.lax.all_gather(partial_value, axis_name='col')  812 us
    all_to_all x1, waiting for transfers between devices, on_device(): lax.all_to_all(local_grad, 'depth', split_axis=0, concat_axis=1, tiled=True)  52.3 us
    all_gather x1, waiting for transfers between devices, on_device(): every_grad = lax.all_gather(grad_out, 'depth', axis=0, tiled=True)  32.8 us
    reduce_sum x1, other arithmetic, finish_rows(): total = jnp.sum(passed, 0)  23.9 us
  transfers between devices with their start and end apart: 4, of which 3 were waited for; matrix products, arithmetic and copies ran while one was open for 6% of the time, Pallas kernels for 0%

profile of v1, /device:TPU:0, one launch (start us, length us, event | category | flops | bytes accessed | tf_op | source)
XLA Modules:
  0.0 1030.7 jit_solution(17031740556547483806)
XLA Ops:
  7.2 0.0 all-gather.4.cloned.1.call-start
  7.2 0.7 all-gather.4.cloned.1.call-update
  7.9 0.0 all-gather.6.cloned.1.call-start
  7.9 32.8 %all-gather.4.cloned.1.call-done = bf16[1024,1536]{1,0:T(8,128)(2,1)} async-done(((bf16[256,1536]{1,0:T(8,128)(2,1)}), bf16[1024,1536]{1,0:T(8,128)(2,1)}) %all-gather.4.cloned.1.call-update) | async-done | bytes 3145744 | tf_op jit(solution)/shard_map/all_gather | solution.py:40
  40.8 16.2 %fusion.15 = f32[1024,3072]{1,0:T(8,128)} fusion(bf16[1024,1536]{1,0:T(8,128)(2,1)} %all-gather.4.cloned.1.call-done, bf16[3072,1536]{1,0:T(8,128)(2,1)} %param.5), kind=kOutput, calls=%fused_computation.21 | convolution fusion | flops 9663676416 | bytes 25165824 | tf_op jit(solution)/shard_map/dot_general | solution.py:22
  57.0 0.0 all-gather.6.cloned.1.call-update
  57.0 8.8 copy.5
  65.8 9.9 copy.6
  75.7 5.6 all-to-all-start
  81.3 811.9 %all-gather.6.cloned.1.call-done = f32[4096,3072]{1,0:T(8,128)} async-done(((f32[1024,3072]{1,0:T(8,128)}), f32[4096,3072]{1,0:T(8,128)}) %all-gather.6.cloned.1.call-update) | async-done | bytes 50331664 | tf_op jit(solution)/shard_map/all_gather | solution.py:34
  893.1 23.9 %reduce_sum.11 = f32[1024,3072]{1,0:T(8,128)} reduce(f32[4,1024,3072]{2,1,0:T(8,128)} %bitcast.29, f32[]{:T(128)} %constant.0.clone.1), dimensions={0}, to_apply=%region_0.0 | reduce | flops 9437184 | bytes 62914564 | tf_op jit(solution)/shard_map/reduce_sum | solution.py:35
  917.1 0.0 all-to-all-done
  917.1 13.3 %fusion.7 = bf16[4,256,3072]{2,1,0:T(8,128)(2,1)} fusion(f32[4,256,3072]{2,1,0:T(8,128)} %bitcast.30, bf16[256,4,3072]{2,0,1:T(8,128)(2,1)} %all-to-all-done), kind=kLoop, calls=%fused_computation.10 | loop fusion | flops 62914560 | bytes 25165824 | tf_op jit(solution)/shard_map/convert_element_type | solution.py:36
  930.4 0.0 copy-start
  930.4 5.7 all-to-all-start.1
  936.1 6.1 fusion.12
  942.2 0.0 copy-done
  942.2 12.1 %convolution_convert_fusion = bf16[3072,1536]{1,0:T(8,128)(2,1)} fusion(bf16[1024,3072]{1,0:T(8,128)(2,1)S(1)} %fusion.12, bf16[1024,1536]{1,0:T(8,128)(2,1)S(1)} %copy-done), kind=kOutput, calls=%fused_computation.20 | convolution fusion | flops 9668395008 | bytes 18874368 | tf_op jit(solution)/shard_map/dot_general | solution.py:28
  954.3 52.3 %all-to-all-done.1 = bf16[4,256,3072]{2,1,0:T(8,128)(2,1)} async-done(((bf16[4,256,3072]{2,1,0:T(8,128)(2,1)}), bf16[4,256,3072]{2,1,0:T(8,128)(2,1)}, u32[]{:S(2)}, u32[]{:S(2)}) %all-to-all-start.1) | async-done | bytes 6291488 | tf_op jit(solution)/shard_map/all_to_all | solution.py:44
  1006.6 8.6 copy.7
  1015.2 8.6 copy.8
Async XLA Ops:
  7.2 33.6 %all-gather.4.cloned.1.call-start = ((), (), s32[]{:S(2)}) async-start(), calls=%async_computation.2 | async-start | bytes 3932160 | tf_op jit(solution)/shard_map/all_gather | solution.py:40
  7.9 885.2 %all-gather.6.cloned.1.call-start = ((), (), s32[]{:S(2)}) async-start(), calls=%async_computation.3 | async-start | bytes 62914560 | tf_op jit(solution)/shard_map/all_gather | solution.py:34
  75.7 841.4 %all-to-all-start = ((bf16[256,4,3072]{2,0,1:T(8,128)(2,1)}), bf16[256,4,3072]{2,0,1:T(8,128)(2,1)}, u32[]{:S(2)}, u32[]{:S(2)}) async-start(bf16[256,4,3072]{2,0,1:T(8,128)(2,1)} %copy.6), calls=%async_computation | async-start | bytes 12582912 | tf_op jit(solution)/shard_map/all_to_all | solution.py:41
  930.4 11.8 %copy-start = (bf16[1024,1536]{1,0:T(8,128)(2,1)S(1)}, bf16[1024,1536]{1,0:T(8,128)(2,1)}, u32[]{:S(2)}) copy-start(bf16[1024,1536]{1,0:T(8,128)(2,1)} %all-gather.4.cloned.1.call-done) | copy-start | bytes 9437188
  930.4 76.2 %all-to-all-start.1 = ((bf16[4,256,3072]{2,1,0:T(8,128)(2,1)}), bf16[4,256,3072]{2,1,0:T(8,128)(2,1)}, u32[]{:S(2)}, u32[]{:S(2)}) async-start(bf16[4,256,3072]{2,1,0:T(8,128)(2,1)} %fusion.7), calls=%async_computation.1 | async-start | bytes 12582912 | tf_op jit(solution)/shard_map/all_to_all | solution.py:44
Sparse Core Ops, SparseCore 0:
  9.5 31.2 all-gather.3
  57.1 835.9 all-gather.5
